TPU v7x, 128 devices: a whole 4x4x4 slice. The times are simulated.
128 devices in a mesh: dp: 1, ep: 128 (over z, y, x, core).
Axes of the slice: x: 4, y: 4, z: 4, core: 2. Of those that a mesh axis runs over, the one named last changes fastest.
Arguments:
- x_tok: bfloat16 [49152, 2048], P(('dp', 'ep'))
- topk_idx: int32 [49152, 8], P(('dp', 'ep'))
- topk_w: float32 [49152, 8], P(('dp', 'ep'))
- w_in: bfloat16 [256, 2048, 512], P('ep')
- w_out: bfloat16 [256, 512, 2048], P('ep')
- shared_in: bfloat16 [2048, 512], replicated
- shared_out: bfloat16 [512, 2048], replicated
Outputs:
- output: bfloat16 [49152, 2048], P(('dp', 'ep'))
All inputs are finite; a program needn't handle non-finite values.
Results may differ from a plain program's by a relative error of at most 0.001.
Values are sent between devices in bfloat16 or wider.
A program may use at most 1 GiB of HBM per device.

v0:
```python
import jax
import jax.numpy as jnp
from jax import lax
from jax.sharding import PartitionSpec as P

LOAD_MULT = 3


def slot_tables(topk_idx, topk_w, num_experts, slot_cap):
    tok_rows, top_k = topk_idx.shape
    expert_hot = (topk_idx[:, :, None] == jnp.arange(num_experts, dtype=jnp.int32)).astype(jnp.int32)
    running = jnp.cumsum(expert_hot.reshape(tok_rows * top_k, num_experts), axis=0)
    slot_pos = jnp.sum(running.reshape(tok_rows, top_k, num_experts) * expert_hot, axis=2) - 1
    slot_hot = (slot_pos[:, :, None] == jnp.arange(slot_cap, dtype=jnp.int32)).astype(jnp.bfloat16)
    gate_hot = expert_hot.astype(jnp.bfloat16) * topk_w.astype(jnp.bfloat16)[:, :, None]
    combine = jnp.einsum('tje,tjc->tec', gate_hot, slot_hot, preferred_element_type=jnp.float32).astype(jnp.bfloat16)
    dispatch = (combine != 0).astype(jnp.bfloat16)
    return combine, dispatch


def solution(mesh):
    group_size = mesh.shape['ep']

    def local_layer(x_loc, idx_loc, gate_loc, w_in, w_out, shared_in, shared_out):
        tok_rows, top_k = idx_loc.shape
        num_experts = w_in.shape[0] * group_size
        slot_cap = min(tok_rows, LOAD_MULT * tok_rows * top_k // num_experts)
        combine, dispatch = slot_tables(idx_loc, gate_loc, num_experts, slot_cap)
        send_rows = jnp.einsum('tec,tm->ecm', dispatch, x_loc, preferred_element_type=jnp.float32).astype(jnp.bfloat16)
        recv_rows = lax.all_to_all(send_rows, 'ep', 0, 1, tiled=True)
        hidden = jax.nn.gelu(jnp.einsum('erm,emf->erf', recv_rows, w_in, preferred_element_type=jnp.float32), approximate=True).astype(jnp.bfloat16)
        expert_out = jnp.einsum('erf,efm->erm', hidden, w_out, preferred_element_type=jnp.float32).astype(jnp.bfloat16)
        back_rows = lax.all_to_all(expert_out, 'ep', 1, 0, tiled=True)
        routed = jnp.einsum('tec,ecm->tm', combine, back_rows, preferred_element_type=jnp.float32)
        shared_hidden = jax.nn.gelu(jnp.dot(x_loc, shared_in, preferred_element_type=jnp.float32), approximate=True).astype(jnp.bfloat16)
        shared_val = jnp.dot(shared_hidden, shared_out, preferred_element_type=jnp.float32)
        return (routed + shared_val).astype(jnp.bfloat16)

    tok_spec = P(('dp', 'ep'), None)
    expert_spec = P('ep', None, None)
    whole_spec = P(None, None)
    return jax.shard_map(local_layer, mesh=mesh, in_specs=(tok_spec, tok_spec, tok_spec, expert_spec, expert_spec, whole_spec, whole_spec), out_specs=tok_spec, check_vma=False)
```

profile of v0, /device:TPU:17, one launch (start us, length us, event | category | flops | bytes accessed | tf_op | source)
XLA Modules:
  0.0 1496.0 jit_solution(15466948649521137334)
XLA Ops:
  0.0 0.0 copy-start
  0.0 1.0 copy.39
  1.0 0.1 eq.53
  1.1 0.1 eq.49
  1.3 0.7 convert_element_type.36
  2.0 0.2 copy.40
  2.1 0.1 copy.43
  2.2 0.5 fusion.22
  2.7 0.0 copy-start.1
  2.7 1.7 copy-done.1
  4.4 2.1 broadcast_add_fusion
  6.5 1.0 copy.44
  7.6 1.9 fusion.20
  9.5 0.1 sub.7
  9.6 0.0 copy-start.2
  9.6 6.3 fusion.26
  15.9 0.0 copy-done.2
  15.9 44.7 %convolution_convert_fusion.1 = bf16[256,36,2048]{2,0,1:T(8,128)(2,1)} fusion(bf16[384,256,36]{1,2,0:T(8,128)(2,1)} %fusion.26, bf16[384,2048]{1,0:T(8,128)(2,1)S(1)} %copy-done.2), kind=kOutput, calls=%fused_computation.4 | convolution fusion | flops 14517927936 | bytes 46399488 | tf_op jit(solution)/shard_map/tec,tm->ecm/dot_general | solution.py:29
  60.6 37.0 %copy.47 = bf16[256,36,2048]{2,1,0:T(8,128)(2,1)} copy(bf16[256,36,2048]{2,0,1:T(8,128)(2,1)} %convolution_convert_fusion.1) | data formatting | bytes 75497472 | tf_op jit(solution)/shard_map/convert_element_type | solution.py:29
  97.6 539.5 %all_to_all.36 = bf16[256,36,2048]{2,1,0:T(8,128)(2,1)} all-to-all(bf16[256,36,2048]{2,1,0:T(8,128)(2,1)} %copy.47), channel_id=1, replica_groups=mesh['dp'=1,'ep'=128] {'ep'}, dimensions={0} | all-to-all | bytes 75497472 | tf_op jit(solution)/shard_map/all_to_all | solution.py:30
  637.1 55.5 %copy.48 = bf16[128,2,36,2048]{3,1,2,0:T(2,128)(2,1)} copy(bf16[128,2,36,2048]{3,2,1,0:T(8,128)(2,1)} %bitcast.33) | data formatting | bytes 75497472 | tf_op jit(solution)/shard_map/all_to_all | solution.py:30
  692.6 65.0 %convolution_convert_fusion = bf16[2,4608,2048]{2,1,0:T(8,128)(2,1)} fusion(bf16[2,512,2048]{2,1,0:T(8,128)(2,1)} %param.11, bf16[2,2048,512]{2,1,0:T(8,128)(2,1)} %param.10, bf16[2,4608,2048]{2,0,1:T(2,128)(2,1)} %bitcast.35), kind=kOutput, calls=%fused_computation.3 | convolution fusion | flops 38716047360 | bytes 83886080 | tf_op jit(solution)/shard_map/erf,efm->erm/dot_general | solution.py:32
  757.6 67.4 %copy.50 = bf16[2,4608,2048]{2,0,1:T(2,128)(2,1)} copy(bf16[2,4608,2048]{2,1,0:T(8,128)(2,1)} %convolution_convert_fusion) | data formatting | bytes 75497472 | tf_op jit(solution)/shard_map/convert_element_type | solution.py:32
  825.0 555.8 %all_to_all.37 = bf16[2,4608,2048]{2,0,1:T(2,128)(2,1)} all-to-all(bf16[2,4608,2048]{2,0,1:T(2,128)(2,1)} %copy.50), channel_id=1, replica_groups=mesh['dp'=1,'ep'=128] {'ep'}, dimensions={1} | all-to-all | bytes 75497472 | tf_op jit(solution)/shard_map/all_to_all | solution.py:33
  1380.7 29.9 %copy.51 = bf16[128,2,36,2048]{3,1,0,2:T(2,128)(2,1)} copy(bf16[128,2,36,2048]{3,1,2,0:T(2,128)(2,1)} %bitcast.34) | data formatting | bytes 75497472 | tf_op jit(solution)/shard_map/all_to_all | solution.py:33
  1410.6 54.4 %all_to_all.33 = bf16[256,36,2048]{2,0,1:T(8,128)(2,1)} reshape(bf16[128,2,36,2048]{3,1,0,2:T(2,128)(2,1)} %copy.51) | data formatting | bytes 75497472 | tf_op jit(solution)/shard_map/all_to_all | solution.py:33
  1464.9 24.9 %fusion.24 = f32[384,2048,1]{1,0,2:T(8,128)} fusion(bf16[256,36,2048]{2,0,1:T(8,128)(2,1)} %all_to_all.33, bf16[384,256,36]{1,2,0:T(8,128)(2,1)} %fusion.26), kind=kOutput, calls=%fused_computation.30 | convolution fusion | flops 14495514624 | bytes 47972352 | tf_op jit(solution)/shard_map/tec,ecm->tm/dot_general | solution.py:34
  1489.9 0.0 copy-done
  1489.9 6.1 fusion.21
  (4 shorter events, 0.1 us)
Async XLA Ops:
  0.0 1489.9 %copy-start = (bf16[512,2048]{1,0:T(8,128)(2,1)S(1)}, bf16[512,2048]{1,0:T(8,128)(2,1)}, u32[]{:S(2)}) copy-start(bf16[512,2048]{1,0:T(8,128)(2,1)} %param.13) | copy-start | bytes 6291460
  2.7 1.7 copy-start.1
  9.6 6.3 copy-start.2
where the time goes:
time: 1510 us; the launch traced here: 1500 us
  blocking collectives  1100 us (73%)
  local copies, waits for them, and re-layouts  248 us (16%)
  matrix products  147 us (10%)
    all_to_all x1, blocking collectives, local_layer(): back_rows = lax.all_to_all(expert_out, 'ep', 1, 0, tiled=True)  556 us
    all_to_all x1, blocking collectives, local_layer(): recv_rows = lax.all_to_all(send_rows, 'ep', 0, 1, tiled=True)  539 us
    all_to_all x2, local copies, waits for them, and re-layouts, local_layer(): back_rows = lax.all_to_all(expert_out, 'ep', 1, 0, tiled=True)  84.2 us
    convert_element_type x1, local copies, waits for them, and re-layouts, local_layer(): jnp.einsum('erf,efm->erm', hidden, w_out, preferred_element_type=jnp.floa...  67.4 us
    dot_general x1, matrix products, local_layer(): jnp.einsum('erf,efm->erm', hidden, w_out, preferred_element_type=jnp.floa...  65 us
    all_to_all x1, local copies, waits for them, and re-layouts, local_layer(): recv_rows = lax.all_to_all(send_rows, 'ep', 0, 1, tiled=True)  55.5 us
    dot_general x1, matrix products, local_layer(): jnp.einsum('tec,tm->ecm', dispatch, x_loc, preferred_element_type=jnp.flo...  44.7 us
    convert_element_type x1, local copies, waits for them, and re-layouts, local_layer(): jnp.einsum('tec,tm->ecm', dispatch, x_loc, preferred_element_type=jnp.flo...  37 us

commit v1 on v0

v1 whole, which is shorter than its diff:
```python
import jax
import jax.numpy as jnp
from jax import lax
from jax.sharding import PartitionSpec as P

LOAD_MULT = 3
BASE_CAP = 12
HOT = 8
TILE = 8
BF16 = jnp.bfloat16
F32 = jnp.float32


def gelu(z):
    return jax.nn.gelu(z, approximate=True)


def slot_tables(topk_idx, topk_w, num_experts, slot_cap):
    tok_rows, top_k = topk_idx.shape
    expert_hot = (topk_idx[:, :, None] == jnp.arange(num_experts, dtype=jnp.int32)).astype(jnp.int32)
    running = jnp.cumsum(expert_hot.reshape(tok_rows * top_k, num_experts), axis=0)
    slot_pos = jnp.sum(running.reshape(tok_rows, top_k, num_experts) * expert_hot, axis=2) - 1
    slot_hot = (slot_pos[:, :, None] == jnp.arange(slot_cap, dtype=jnp.int32)).astype(BF16)
    gate_hot = expert_hot.astype(BF16) * topk_w.astype(BF16)[:, :, None]
    combine = jnp.einsum('tje,tjc->tec', gate_hot, slot_hot, preferred_element_type=F32).astype(BF16)
    dispatch = (combine != 0).astype(BF16)
    return combine, dispatch


def solution(mesh):
    group_size = mesh.shape['ep']
    members = group_size // HOT
    hot_teams = [[h * members + r for r in range(members)] for h in range(HOT)]
    hot_lanes = [[h * members + r for h in range(HOT)] for r in range(members)]

    def wide_layer(x_loc, idx_loc, gate_loc, w_in, w_out, shared_val):
        tok_rows, top_k = idx_loc.shape
        num_experts = w_in.shape[0] * group_size
        slot_cap = min(tok_rows, LOAD_MULT * tok_rows * top_k // num_experts)
        combine, dispatch = slot_tables(idx_loc, gate_loc, num_experts, slot_cap)
        send_rows = jnp.einsum('tec,tm->ecm', dispatch, x_loc, preferred_element_type=F32).astype(BF16)
        recv_rows = lax.all_to_all(send_rows, 'ep', 0, 1, tiled=True)
        hidden = gelu(jnp.einsum('erm,emf->erf', recv_rows, w_in, preferred_element_type=F32)).astype(BF16)
        expert_out = jnp.einsum('erf,efm->erm', hidden, w_out, preferred_element_type=F32).astype(BF16)
        back_rows = lax.all_to_all(expert_out, 'ep', 1, 0, tiled=True)
        routed = jnp.einsum('tec,ecm->tm', combine, back_rows, preferred_element_type=F32)
        return (routed + shared_val).astype(BF16)

    def local_layer(x_loc, idx_loc, gate_loc, w_in, w_out, shared_in, shared_out):
        tok_rows, top_k = idx_loc.shape
        d_model = x_loc.shape[1]
        per_dev = w_in.shape[0]
        num_experts = per_dev * group_size
        slot_cap = min(tok_rows, LOAD_MULT * tok_rows * top_k // num_experts)
        base_cap = min(BASE_CAP, slot_cap)
        over_cap = slot_cap - base_cap
        me = lax.axis_index('ep')

        expert_ids = jnp.arange(num_experts, dtype=jnp.int32)
        pick = idx_loc[:, :, None] == expert_ids
        picked = jnp.any(pick, axis=1)
        gate_rows = gate_loc.astype(BF16).astype(F32)
        gates = jnp.sum(jnp.where(pick, gate_rows[:, :, None], 0.0), axis=1).astype(BF16)
        ones = picked.astype(BF16)
        before = (jnp.arange(tok_rows)[:, None] > jnp.arange(tok_rows)[None, :]).astype(BF16)
        rank = jnp.dot(before, ones, preferred_element_type=F32)
        slot = jnp.where(picked, rank, -1.0).astype(BF16)

        counts = jnp.sum(picked.astype(jnp.int32), axis=0)
        peak = lax.pmax(counts, 'ep')
        over = peak > base_cap
        over_rank = jnp.cumsum(over.astype(jnp.int32)) - 1
        fits = jnp.sum(over.astype(jnp.int32)) <= HOT
        hot_sel = (over[:, None] & (over_rank[:, None] == jnp.arange(HOT, dtype=jnp.int32))).astype(BF16)

        mine = lax.dynamic_slice(hot_sel, (me * per_dev, 0), (per_dev, HOT))

        def to_team(w):
            rows, cols = w.shape[1:]
            spread = jnp.zeros((HOT, rows, cols), BF16)
            for k in range(per_dev):
                spread = jnp.where((mine[k] != 0)[:, None, None], w[k][None], spread)
            piece = lax.psum_scatter(spread.reshape(HOT * rows, cols), 'ep', scatter_dimension=0, tiled=True)
            return lax.all_gather(piece, 'ep', axis_index_groups=hot_teams, axis=0, tiled=True)

        hot_in = to_team(w_in)
        hot_out = to_team(w_out)

        base_rows = num_experts * base_cap
        owner = jnp.arange(base_rows, dtype=jnp.int32) // base_cap
        place = (jnp.arange(base_rows, dtype=jnp.int32) % base_cap).astype(F32)
        repeat = (expert_ids[:, None] == owner[None, :]).astype(BF16)
        slot_of = jnp.dot(slot, repeat, preferred_element_type=F32)
        gate_of = jnp.dot(gates, repeat, preferred_element_type=F32)
        base_unit = (slot_of == place).astype(BF16)
        base_gate = jnp.where(slot_of == place, gate_of, 0.0).astype(BF16)

        hot_rows = HOT * over_cap
        hot_owner = jnp.arange(hot_rows, dtype=jnp.int32) // over_cap
        hot_place = (jnp.arange(hot_rows, dtype=jnp.int32) % over_cap + base_cap).astype(F32)
        hot_repeat = (jnp.arange(HOT, dtype=jnp.int32)[:, None] == hot_owner[None, :]).astype(BF16)
        hot_map = jnp.dot(hot_sel, hot_repeat, preferred_element_type=F32).astype(BF16)
        hot_slot_of = jnp.dot(slot, hot_map, preferred_element_type=F32)
        hot_gate_of = jnp.dot(gates, hot_map, preferred_element_type=F32)
        hot_unit = (hot_slot_of == hot_place).astype(BF16)
        hot_gate = jnp.where(hot_slot_of == hot_place, hot_gate_of, 0.0).astype(BF16)

        send = jnp.einsum('tr,tm->rm', base_unit, x_loc, preferred_element_type=F32).astype(BF16)
        recv = lax.all_to_all(send.reshape(group_size, per_dev * base_cap, d_model), 'ep', 0, 0, tiled=True)
        hot_send = jnp.einsum('tr,tm->rm', hot_unit, x_loc, preferred_element_type=F32).astype(BF16)
        hot_recv = lax.all_to_all(hot_send.reshape(HOT, over_cap, d_model), 'ep', 0, 0, axis_index_groups=hot_lanes, tiled=True)

        def ffn(rows, first, second):
            hidden = gelu(jnp.dot(rows, first, preferred_element_type=F32)).astype(BF16)
            return jnp.dot(hidden, second, preferred_element_type=F32)

        span = 2 * TILE
        first = ffn(recv[:, :span].reshape(group_size * span, d_model), w_in[0], w_out[0]).astype(BF16)
        second = ffn(recv[:, TILE:].reshape(group_size * span, d_model), w_in[1], w_out[1]).astype(BF16)
        first = first.reshape(group_size, span, d_model)
        second = second.reshape(group_size, span, d_model)
        middle = jnp.where(jnp.arange(TILE)[None, :, None] < base_cap - TILE, first[:, TILE:], second[:, :TILE])
        done = jnp.concatenate([first[:, :TILE], middle, second[:, TILE:]], axis=1)
        hot_done = ffn(hot_recv.reshape(hot_rows, d_model), hot_in, hot_out).astype(BF16)

        back = lax.all_to_all(done, 'ep', 0, 0, tiled=True).reshape(base_rows, d_model)
        hot_back = lax.all_to_all(hot_done.reshape(HOT, over_cap, d_model), 'ep', 0, 0, axis_index_groups=hot_lanes, tiled=True)
        hot_back = hot_back.reshape(hot_rows, d_model)

        shared_val = ffn(x_loc, shared_in, shared_out)
        routed = jnp.dot(base_gate, back, preferred_element_type=F32) + jnp.dot(hot_gate, hot_back, preferred_element_type=F32)
        tight = (routed + shared_val).astype(BF16)
        return lax.cond(
            fits,
            lambda *_: tight,
            lambda *args: wide_layer(*args),
            x_loc, idx_loc, gate_loc, w_in, w_out, shared_val,
        )

    tok_spec = P(('dp', 'ep'), None)
    expert_spec = P('ep', None, None)
    whole_spec = P(None, None)
    return jax.shard_map(local_layer, mesh=mesh, in_specs=(tok_spec, tok_spec, tok_spec, expert_spec, expert_spec, whole_spec, whole_spec), out_specs=tok_spec, check_vma=False)
```

time: 1510 us -> 1620 us (1.073)
  waiting for transfers between devices: 0 us -> 1350 us
  blocking collectives: 1100 us -> 66.2 us
  local copies, waits for them, and re-layouts: 248 us -> 17.4 us
  matrix products: 147 us -> 72.5 us
  other arithmetic: 5.23 us -> 43.1 us
  starting transfers between devices: 0 us -> 36.6 us
    all_to_all x2 -> x0, blocking collectives: 1100 us -> none  [the longest x1 556 us: local_layer(): back_rows = lax.all_to_all(expert_out, 'ep', 1, 0, tiled=True)]
    reduce_scatter x0 -> x2, waiting for transfers between devices: none -> 1060 us  [to_team(): lax.psum_scatter(spread.reshape(HOT * rows, cols), 'ep', scatter_dimensio...]
    all_to_all x0 -> x4, waiting for transfers between devices: none -> 184 us  [the longest x1 183 us: local_layer(): lax.all_to_all(send.reshape(group_size, per_dev * base_cap, d_model), 'ep...]
    all_to_all x3 -> x0, local copies, waits for them, and re-layouts: 140 us -> none  [the longest x2 84.2 us: local_layer(): back_rows = lax.all_to_all(expert_out, 'ep', 1, 0, tiled=True)]
    all_gather x0 -> x2, waiting for transfers between devices: none -> 115 us  [to_team(): lax.all_gather(piece, 'ep', axis_index_groups=hot_teams, axis=0, tiled=True)]
    convert_element_type x3 -> x1, local copies, waits for them, and re-layouts: 105 us -> 0.12 us  [local_layer(): gate_rows = gate_loc.astype(BF16).astype(F32)]
    dot_general x5 -> x14, matrix products: 147 us -> 72.5 us  [the longest x4 29.6 us: ffn(): return jnp.dot(hidden, second, preferred_element_type=F32)]
    pmax x0 -> x1, blocking collectives: none -> 66.2 us  [local_layer(): peak = lax.pmax(counts, 'ep')]
  transfers between devices with their start and end apart: 0 -> 8, of which waited for: 0 -> 6; matrix products, arithmetic and copies ran while one was open for 0% -> 6% of each run, Pallas kernels for 0% -> 0%
where the time goes in v1:
time: 1620 us; the launch traced here: 1610 us
  waiting for transfers between devices  1350 us (83%)
  matrix products  72.5 us (4%)
  blocking collectives  66.2 us (4%)
  other arithmetic  43.1 us (3%)
  starting transfers between devices  36.6 us (2%)
  local copies, waits for them, and re-layouts  17.4 us (1%)
    reduce_scatter x2, waiting for transfers between devices, to_team(): lax.psum_scatter(spread.reshape(HOT * rows, cols), 'ep', scatter_dimensio...  1060 us
    all_to_all x1, waiting for transfers between devices, local_layer(): lax.all_to_all(send.reshape(group_size, per_dev * base_cap, d_model), 'ep...  183 us
    all_gather x2, waiting for transfers between devices, to_team(): lax.all_gather(piece, 'ep', axis_index_groups=hot_teams, axis=0, tiled=True)  115 us
    pmax x1, blocking collectives, local_layer(): peak = lax.pmax(counts, 'ep')  66.2 us
  transfers between devices with their start and end apart: 8, of which 6 were waited for; matrix products, arithmetic and copies ran while one was open for 6% of the time, Pallas kernels for 0%

profile of v1, /device:TPU:17, one launch (start us, length us, event | category | flops | bytes accessed | tf_op | source)
XLA Modules:
  0.0 1605.4 jit_solution(3885165588056717533)
XLA Ops:
  7.5 2.1 fusion.55
  9.7 66.2 %pmax.7 = s32[256]{0:T(256)S(1)} all-reduce(s32[256]{0:T(256)S(1)} %convert_reduce_fusion), channel_id=1, replica_groups=mesh['dp'=1,'ep'=128] {'ep'}, use_global_device_ids=true, to_apply=%region_2.3 | all-reduce | flops 256 | bytes 2048 | tf_op jit(solution)/shard_map/pmax | solution.py:70
  76.9 4.4 slice_bitcast_fusion.2
  81.3 17.3 %fusion.38 = bf16[16384,512]{1,0:T(8,128)(2,1)} fusion(pred[16384]{0:T(1024)(128)(4,1)S(1)} %bitcast.115, pred[16384]{0:T(1024)(128)(4,1)S(1)} %bitcast.116, bf16[2048,512]{1,0:T(8,128)(2,1)} %get-tuple-element.66, bf16[2048,512]{1,0:T(8,128)(2,1)} %get-tuple-element.65), kind=kLoop, calls=%fused_computation.49 | loop fusion | flops 16777216 | bytes 21004288 | tf_op jit(solution)/shard_map/jit(_where)/select_n | solution.py:82
  98.8 2.7 slice_bitcast_fusion.1
  101.6 8.1 fusion.37
  110.0 1.3 convolution_compare_fusion
  111.4 9.6 convolution_convert_fusion.2
  121.0 7.3 all-to-all-start.2
  129.0 2.9 convolution_convert_fusion.6
  131.9 183.0 %all-to-all-done.2 = bf16[128,24,2048]{2,1,0:T(8,128)(2,1)} async-done(((bf16[128,24,2048]{2,1,0:T(8,128)(2,1)}), bf16[128,24,2048]{2,1,0:T(8,128)(2,1)}, u32[]{:S(2)}, u32[]{:S(2)}) %all-to-all-start.2) | async-done | bytes 12582944 | tf_op jit(solution)/shard_map/all_to_all | solution.py:109
  314.8 11.5 all-to-all-start.4
  326.4 6.9 fusion.138
  333.5 6.4 fusion.137
  339.8 9.8 convolution_convert_fusion.3
  349.6 6.3 fusion.136
  355.9 9.8 convolution_convert_fusion.4
  365.6 6.4 fusion.139
  372.0 5.6 pad_maximum_fusion
  377.6 10.6 all-to-all-start.3
  388.2 387.0 %reduce-scatter.3.cloned.1.call-done = bf16[128,512]{1,0:T(8,128)(2,1)} async-done(((bf16[16384,512]{1,0:T(8,128)(2,1)}), bf16[128,512]{1,0:T(8,128)(2,1)}) %reduce-scatter.3.cloned.1.call-update) | async-done | bytes 131088 | tf_op jit(solution)/shard_map/reduce_scatter | solution.py:83
  775.5 668.0 %reduce-scatter.5.cloned.1.call-done = bf16[32,2048]{1,0:T(8,128)(2,1)} async-done(((bf16[4096,2048]{1,0:T(8,128)(2,1)}), bf16[32,2048]{1,0:T(8,128)(2,1)}) %reduce-scatter.5.cloned.1.call-update) | async-done | bytes 131088 | tf_op jit(solution)/shard_map/reduce_scatter | solution.py:83
  1445.0 5.8 fusion.87
  1450.8 2.2 select_reduce_fusion
  1453.0 79.8 %all-gather.3.cloned.1.call-done = bf16[2048,512]{1,0:T(8,128)(2,1)} async-done(((bf16[128,512]{1,0:T(8,128)(2,1)}), bf16[2048,512]{1,0:T(8,128)(2,1)}) %all-gather.3.cloned.1.call-update) | async-done | bytes 2097168 | tf_op jit(solution)/shard_map/all_gather | solution.py:84
  1532.8 35.3 %all-gather.5.cloned.1.call-done = bf16[512,2048]{1,0:T(8,128)(2,1)} async-done(((bf16[32,2048]{1,0:T(8,128)(2,1)}), bf16[512,2048]{1,0:T(8,128)(2,1)}) %all-gather.5.cloned.1.call-update) | async-done | bytes 2097168 | tf_op jit(solution)/shard_map/all_gather | solution.py:84
  1568.2 4.3 convolution_convert_fusion.5
  1572.4 6.8 all-to-all-start.5
  1579.3 10.9 fusion.70
  1590.8 4.8 add_convert_fusion
  1595.6 1.1 conditional.1
  1596.8 1.6 copy-done.1
  (54 shorter events, 5.1 us)
Async XLA Ops:
  6.5 1438.5 %copy-start = (bf16[512,2048]{1,0:T(8,128)(2,1)S(1)}, bf16[512,2048]{1,0:T(8,128)(2,1)}, u32[]{:S(2)}) copy-start(bf16[512,2048]{1,0:T(8,128)(2,1)} %param.15) | copy-start | bytes 6291460
  6.5 768.7 %reduce-scatter.3.cloned.1.call-start = ((), (), s32[]{:S(2)}) async-start(), calls=%async_computation.8 | async-start | bytes 16908288 | tf_op jit(solution)/shard_map/reduce_scatter | solution.py:83
  98.7 1344.9 %reduce-scatter.5.cloned.1.call-start = ((), (), s32[]{:S(2)}) async-start(), calls=%async_computation.10 | async-start | bytes 16908288 | tf_op jit(solution)/shard_map/reduce_scatter | solution.py:83
  110.0 1.4 copy-start.5
  111.4 9.6 copy-start.9
  121.0 193.8 %all-to-all-start.2 = ((bf16[128,24,2048]{2,1,0:T(8,128)(2,1)}), bf16[128,24,2048]{2,1,0:T(8,128)(2,1)}, u32[]{:S(2)}, u32[]{:S(2)}) async-start(bf16[128,24,2048]{2,1,0:T(8,128)(2,1)} %bitcast.108), calls=%async_computation.2 | async-start | bytes 25165824 | tf_op jit(solution)/shard_map/all_to_all | solution.py:109
  314.8 62.8 %all-to-all-start.4 = ((bf16[8,24,2048]{2,1,0:T(8,128)(2,1)}), bf16[8,24,2048]{2,1,0:T(8,128)(2,1)S(1)}, u32[]{:S(2)}, u32[]{:S(2)}) async-start(bf16[8,24,2048]{2,1,0:T(8,128)(2,1)} %bitcast.22), calls=%async_computation.4 | async-start | bytes 1572864 | tf_op jit(solution)/shard_map/all_to_all | solution.py:111
  326.4 7.1 copy-start.3
  333.5 6.4 copy-start.4
  377.6 1066.0 %copy-start.8 = (f32[384,8]{0,1:T(8,128)S(1)}, f32[384,8]{0,1:T(8,128)}, u32[]{:S(2)}) copy-start(f32[384,8]{0,1:T(8,128)} %param.11) | copy-start | bytes 36868
  377.6 1194.8 %all-to-all-start.3 = ((bf16[128,24,2048]{2,1,0:T(8,128)(2,1)}), bf16[128,24,2048]{2,1,0:T(8,128)(2,1)}, u32[]{:S(2)}, u32[]{:S(2)}) async-start(bf16[128,24,2048]{2,1,0:T(8,128)(2,1)} %pad_maximum_fusion), calls=%async_computation.3 | async-start | bytes 25165824 | tf_op jit(solution)/shard_map/all_to_all | solution.py:126
  388.2 1144.6 %all-gather.3.cloned.1.call-start = ((), (), s32[]{:S(2)}) async-start(), calls=%async_computation.9 | async-start | bytes 2228224 | tf_op jit(solution)/shard_map/all_gather | solution.py:84
  775.3 792.9 %all-gather.5.cloned.1.call-start = ((), (), s32[]{:S(2)}) async-start(), calls=%async_computation.11 | async-start | bytes 2228224 | tf_op jit(solution)/shard_map/all_gather | solution.py:84
  1572.4 18.3 %all-to-all-start.5 = ((bf16[8,24,2048]{2,1,0:T(8,128)(2,1)}), bf16[8,24,2048]{2,1,0:T(8,128)(2,1)S(1)}, u32[]{:S(2)}, u32[]{:S(2)}) async-start(bf16[8,24,2048]{2,1,0:T(8,128)(2,1)} %bitcast.30), calls=%async_computation.7 | async-start | bytes 1572864 | tf_op jit(solution)/shard_map/all_to_all | solution.py:127
  1579.3 11.5 copy-start.7
  1596.7 1.6 copy-start.1
Sparse Core Ops, SparseCore 0:
  98.8 676.4 reduce-scatter.2
  777.6 665.8 reduce-scatter.4
  1445.2 87.5 all-gather.2
  1534.4 33.7 all-gather.4

commit v2 on v1

--- a/solution.py
+++ b/solution.py
@@ -1,14 +1,21 @@
+import functools
+
 import jax
 import jax.numpy as jnp
 from jax import lax
+from jax.experimental import pallas as pl
+from jax.experimental.pallas import tpu as pltpu
 from jax.sharding import PartitionSpec as P
 
 LOAD_MULT = 3
 BASE_CAP = 12
 HOT = 8
+CORES = 2
 TILE = 8
+STRIDE = 37
 BF16 = jnp.bfloat16
 F32 = jnp.float32
+MESH = pl.DeviceIdType.MESH
 
 
 def gelu(z):
@@ -27,11 +34,173 @@
     return combine, dispatch
 
 
+def send_to(src, dst, send_sem, recv_sem, peer):
+    return pltpu.make_async_remote_copy(
+        src_ref=src, dst_ref=dst, send_sem=send_sem, recv_sem=recv_sem,
+        device_id={'ep': peer}, device_id_type=MESH,
+    )
+
+
+def peer_of(me, step, n):
+    return lax.rem(me + step * STRIDE, n)
+
+
+def wait_bytes(like_src, like_dst, sem):
+    pltpu.make_async_copy(like_src, like_dst, sem).wait()
+
+
+def counts_kernel(n, mine, peak, table, send_sem, recv_sem, own_sem):
+    me = lax.axis_index('ep')
+    own = pltpu.make_async_copy(mine, table.at[me], own_sem)
+    own.start()
+
+    def start(step, carry):
+        send_to(mine, table.at[me], send_sem, recv_sem, peer_of(me, step, n)).start()
+        return carry
+
+    lax.fori_loop(1, n, start, 0)
+    own.wait()
+    wait_bytes(table.at[pl.ds(0, n - 1)], table.at[pl.ds(0, n - 1)], recv_sem)
+    wait_bytes(table.at[pl.ds(0, n - 1)], table.at[pl.ds(0, n - 1)], send_sem)
+    peak[...] = jnp.max(table[...], axis=0)
+
+
+def hot_rows_out(me, hot, members, src, dst, send_sem, recv_sem, own_sem):
+    team, lane = me // members, lax.rem(me, members)
+    pltpu.make_async_copy(src.at[team], dst.at[team], own_sem).start()
+    for step in range(1, hot):
+        other = lax.rem(team + step, hot)
+        send_to(src.at[other], dst.at[team], send_sem, recv_sem, other * members + lane).start()
+
+
+def hot_rows_wait(hot, src, dst, send_sem, recv_sem, own_sem):
+    wait_bytes(src.at[0], dst.at[0], own_sem)
+    wait_bytes(src.at[pl.ds(0, hot - 1)], dst.at[pl.ds(0, hot - 1)], recv_sem)
+    wait_bytes(src.at[pl.ds(0, hot - 1)], dst.at[pl.ds(0, hot - 1)], send_sem)
+
+
+def dispatch_kernel(
+    n, hot, source, rows, hot_rows, slices, recv, hot_recv, team_w,
+    landed, chosen, base_sems, hot_sems, slice_sems, team_sems,
+):
+    me = lax.axis_index('ep')
+    members = n // hot
+
+    def scatter(step, carry):
+        peer = peer_of(me, step, n)
+        send_to(slices.at[peer], landed.at[me], slice_sems.at[0], slice_sems.at[1], peer).start()
+        return carry
+
+    def base(step, carry):
+        peer = peer_of(me, step, n)
+        send_to(rows.at[peer], recv.at[me], base_sems.at[0], base_sems.at[1], peer).start()
+        return carry
+
+    def spread(step, carry):
+        peer = peer_of(me, step, n)
+        send_to(chosen.at[peer // members], team_w.at[me], team_sems.at[0], team_sems.at[1], peer).start()
+        return carry
+
+    lax.fori_loop(1, n, scatter, 0)
+    pltpu.make_async_copy(slices.at[me], landed.at[me], slice_sems.at[2]).start()
+    hot_rows_out(me, hot, members, hot_rows, hot_recv, hot_sems.at[0], hot_sems.at[1], hot_sems.at[2])
+    pltpu.make_async_copy(rows.at[me], recv.at[me], base_sems.at[2]).start()
+    half = n // 2
+    lax.fori_loop(1, half, base, 0)
+
+    wait_bytes(slices.at[0], landed.at[0], slice_sems.at[2])
+    wait_bytes(slices.at[pl.ds(0, n - 1)], landed.at[pl.ds(0, n - 1)], slice_sems.at[1])
+    for h in range(hot):
+        chosen[h] = landed[source[h]]
+    lax.fori_loop(half, n, base, 0)
+    pltpu.make_async_copy(chosen.at[me // members], team_w.at[me], team_sems.at[2]).start()
+    lax.fori_loop(1, n, spread, 0)
+
+    wait_bytes(slices.at[pl.ds(0, n - 1)], landed.at[pl.ds(0, n - 1)], slice_sems.at[0])
+    hot_rows_wait(hot, hot_rows, hot_recv, hot_sems.at[0], hot_sems.at[1], hot_sems.at[2])
+    wait_bytes(rows.at[0], recv.at[0], base_sems.at[2])
+    wait_bytes(rows.at[pl.ds(0, n - 1)], recv.at[pl.ds(0, n - 1)], base_sems.at[1])
+    wait_bytes(rows.at[pl.ds(0, n - 1)], recv.at[pl.ds(0, n - 1)], base_sems.at[0])
+    wait_bytes(chosen.at[0], team_w.at[0], team_sems.at[2])
+    wait_bytes(slices.at[pl.ds(0, n - 1)], team_w.at[pl.ds(0, n - 1)], team_sems.at[1])
+    wait_bytes(slices.at[pl.ds(0, n - 1)], team_w.at[pl.ds(0, n - 1)], team_sems.at[0])
+
+
+def return_kernel(n, hot, rows, hot_rows, recv, hot_recv, base_sems, hot_sems):
+    me = lax.axis_index('ep')
+    members = n // hot
+
+    def base(step, carry):
+        peer = peer_of(me, step, n)
+        send_to(rows.at[peer], recv.at[me], base_sems.at[0], base_sems.at[1], peer).start()
+        return carry
+
+    hot_rows_out(me, hot, members, hot_rows, hot_recv, hot_sems.at[0], hot_sems.at[1], hot_sems.at[2])
+    pltpu.make_async_copy(rows.at[me], recv.at[me], base_sems.at[2]).start()
+    lax.fori_loop(1, n, base, 0)
+    hot_rows_wait(hot, hot_rows, hot_recv, hot_sems.at[0], hot_sems.at[1], hot_sems.at[2])
+    wait_bytes(rows.at[0], recv.at[0], base_sems.at[2])
+    wait_bytes(rows.at[pl.ds(0, n - 1)], recv.at[pl.ds(0, n - 1)], base_sems.at[1])
+    wait_bytes(rows.at[pl.ds(0, n - 1)], recv.at[pl.ds(0, n - 1)], base_sems.at[0])
+
+
+ANY = pl.BlockSpec(memory_space=pl.ANY)
+VMEM = pl.BlockSpec(memory_space=pltpu.VMEM)
+SMEM = pl.BlockSpec(memory_space=pltpu.SMEM)
+
+
+def like(x):
+    return jax.ShapeDtypeStruct(x.shape, x.dtype)
+
+
+def exchange_counts(n, counts):
+    lanes = min(counts.size, 128)
+    shape = (counts.size // lanes, lanes)
+    mine = counts.reshape(shape)
+    peak = pl.pallas_call(
+        functools.partial(counts_kernel, n),
+        out_shape=like(mine),
+        in_specs=[VMEM],
+        out_specs=VMEM,
+        scratch_shapes=[pltpu.VMEM((n,) + shape, jnp.int32)] + [pltpu.SemaphoreType.DMA] * 3,
+        compiler_params=pltpu.CompilerParams(has_side_effects=True),
+        name='counts',
+    )(mine)
+    return peak.reshape(counts.shape)
+
+
+def dispatch_rows(n, source, rows, hot_rows, slices):
+    sems = pltpu.SemaphoreType.DMA((3,))
+    return pl.pallas_call(
+        functools.partial(dispatch_kernel, n, HOT),
+        out_shape=(like(rows), like(hot_rows), like(slices)),
+        in_specs=[SMEM, ANY, ANY, ANY],
+        out_specs=(ANY, ANY, ANY),
+        scratch_shapes=[
+            pltpu.VMEM(slices.shape, BF16),
+            pltpu.VMEM((HOT,) + slices.shape[1:], BF16),
+            sems, sems, sems, sems,
+        ],
+        compiler_params=pltpu.CompilerParams(has_side_effects=True),
+        name='dispatch',
+    )(source, rows, hot_rows, slices)
+
+
+def return_rows(n, rows, hot_rows):
+    sems = pltpu.SemaphoreType.DMA((3,))
+    return pl.pallas_call(
+        functools.partial(return_kernel, n, HOT),
+        out_shape=(like(rows), like(hot_rows)),
+        in_specs=[ANY, ANY],
+        out_specs=(ANY, ANY),
+        scratch_shapes=[sems, sems],
+        compiler_params=pltpu.CompilerParams(has_side_effects=True),
+        name='collect',
+    )(rows, hot_rows)
+
+
 def solution(mesh):
     group_size = mesh.shape['ep']
-    members = group_size // HOT
-    hot_teams = [[h * members + r for r in range(members)] for h in range(HOT)]
-    hot_lanes = [[h * members + r for h in range(HOT)] for r in range(members)]
 
     def wide_layer(x_loc, idx_loc, gate_loc, w_in, w_out, shared_val):
         tok_rows, top_k = idx_loc.shape
@@ -49,12 +218,19 @@
     def local_layer(x_loc, idx_loc, gate_loc, w_in, w_out, shared_in, shared_out):
         tok_rows, top_k = idx_loc.shape
         d_model = x_loc.shape[1]
+        ff_dim = w_in.shape[2]
         per_dev = w_in.shape[0]
+        per_chip = per_dev * CORES
         num_experts = per_dev * group_size
         slot_cap = min(tok_rows, LOAD_MULT * tok_rows * top_k // num_experts)
         base_cap = min(BASE_CAP, slot_cap)
         over_cap = slot_cap - base_cap
         me = lax.axis_index('ep')
+        chip, core = me // CORES, me % CORES
+
+        partner = [(i, i ^ 1) for i in range(group_size)]
+        other_in = lax.ppermute(w_in, 'ep', partner)
+        other_out = lax.ppermute(w_out, 'ep', partner)
 
         expert_ids = jnp.arange(num_experts, dtype=jnp.int32)
         pick = idx_loc[:, :, None] == expert_ids
@@ -67,24 +243,31 @@
         slot = jnp.where(picked, rank, -1.0).astype(BF16)
 
         counts = jnp.sum(picked.astype(jnp.int32), axis=0)
-        peak = lax.pmax(counts, 'ep')
-        over = peak > base_cap
-        over_rank = jnp.cumsum(over.astype(jnp.int32)) - 1
-        fits = jnp.sum(over.astype(jnp.int32)) <= HOT
-        hot_sel = (over[:, None] & (over_rank[:, None] == jnp.arange(HOT, dtype=jnp.int32))).astype(BF16)
-
-        mine = lax.dynamic_slice(hot_sel, (me * per_dev, 0), (per_dev, HOT))
-
-        def to_team(w):
-            rows, cols = w.shape[1:]
-            spread = jnp.zeros((HOT, rows, cols), BF16)
-            for k in range(per_dev):
-                spread = jnp.where((mine[k] != 0)[:, None, None], w[k][None], spread)
-            piece = lax.psum_scatter(spread.reshape(HOT * rows, cols), 'ep', scatter_dimension=0, tiled=True)
-            return lax.all_gather(piece, 'ep', axis_index_groups=hot_teams, axis=0, tiled=True)
-
-        hot_in = to_team(w_in)
-        hot_out = to_team(w_out)
+        peak = exchange_counts(group_size, counts)
+        over = (peak > base_cap).astype(jnp.int32)
+        over_rank = jnp.cumsum(over) - 1
+        by_chip = over.reshape(group_size // CORES, per_chip)
+        chip_rank = jnp.minimum(jnp.cumsum(by_chip, axis=1) - 1, CORES - 1).reshape(num_experts)
+        fits = (jnp.sum(over) <= HOT) & (jnp.max(jnp.sum(by_chip, axis=1)) <= CORES)
+        hot_sel = (over[:, None] > 0) & (over_rank[:, None] == jnp.arange(HOT, dtype=jnp.int32))
+        holder = expert_ids // per_chip * CORES + chip_rank
+        source = jnp.sum(jnp.where(hot_sel, holder[:, None], 0), axis=0)
+        hot_sel = hot_sel.astype(BF16)
+
+        local_over = lax.dynamic_slice(over, (chip * per_chip,), (per_chip,))
+        local_rank = lax.dynamic_slice(chip_rank, (chip * per_chip,), (per_chip,))
+        offered = (local_over > 0) & (local_rank == core)
+        which = jnp.sum(jnp.where(offered, jnp.arange(per_chip, dtype=jnp.int32), 0))
+        is_mine = which // per_dev == core
+        which = which % per_dev
+
+        def pick_weight(own, other):
+            own = lax.dynamic_index_in_dim(own, which, 0, keepdims=False)
+            other = lax.dynamic_index_in_dim(other, which, 0, keepdims=False)
+            return jnp.where(is_mine, own, other)
+
+        packed = jnp.concatenate([pick_weight(w_in, other_in).reshape(ff_dim, d_model), pick_weight(w_out, other_out)])
+        slices = packed.reshape(group_size, 2 * ff_dim // group_size, d_model)
 
         base_rows = num_experts * base_cap
         owner = jnp.arange(base_rows, dtype=jnp.int32) // base_cap
@@ -95,9 +278,9 @@
         base_unit = (slot_of == place).astype(BF16)
         base_gate = jnp.where(slot_of == place, gate_of, 0.0).astype(BF16)
 
-        hot_rows = HOT * over_cap
-        hot_owner = jnp.arange(hot_rows, dtype=jnp.int32) // over_cap
-        hot_place = (jnp.arange(hot_rows, dtype=jnp.int32) % over_cap + base_cap).astype(F32)
+        hot_count = HOT * over_cap
+        hot_owner = jnp.arange(hot_count, dtype=jnp.int32) // over_cap
+        hot_place = (jnp.arange(hot_count, dtype=jnp.int32) % over_cap + base_cap).astype(F32)
         hot_repeat = (jnp.arange(HOT, dtype=jnp.int32)[:, None] == hot_owner[None, :]).astype(BF16)
         hot_map = jnp.dot(hot_sel, hot_repeat, preferred_element_type=F32).astype(BF16)
         hot_slot_of = jnp.dot(slot, hot_map, preferred_element_type=F32)
@@ -106,9 +289,13 @@
         hot_gate = jnp.where(hot_slot_of == hot_place, hot_gate_of, 0.0).astype(BF16)
 
         send = jnp.einsum('tr,tm->rm', base_unit, x_loc, preferred_element_type=F32).astype(BF16)
-        recv = lax.all_to_all(send.reshape(group_size, per_dev * base_cap, d_model), 'ep', 0, 0, tiled=True)
         hot_send = jnp.einsum('tr,tm->rm', hot_unit, x_loc, preferred_element_type=F32).astype(BF16)
-        hot_recv = lax.all_to_all(hot_send.reshape(HOT, over_cap, d_model), 'ep', 0, 0, axis_index_groups=hot_lanes, tiled=True)
+        recv, hot_recv, team_w = dispatch_rows(
+            group_size, source,
+            send.reshape(group_size, per_dev * base_cap, d_model), hot_send.reshape(HOT, over_cap, d_model), slices,
+        )
+        team_w = team_w.reshape(2 * ff_dim, d_model)
+        hot_in, hot_out = team_w[:ff_dim].reshape(d_model, ff_dim), team_w[ff_dim:]
 
         def ffn(rows, first, second):
             hidden = gelu(jnp.dot(rows, first, preferred_element_type=F32)).astype(BF16)
@@ -121,11 +308,11 @@
         second = second.reshape(group_size, span, d_model)
         middle = jnp.where(jnp.arange(TILE)[None, :, None] < base_cap - TILE, first[:, TILE:], second[:, :TILE])
         done = jnp.concatenate([first[:, :TILE], middle, second[:, TILE:]], axis=1)
-        hot_done = ffn(hot_recv.reshape(hot_rows, d_model), hot_in, hot_out).astype(BF16)
-
-        back = lax.all_to_all(done, 'ep', 0, 0, tiled=True).reshape(base_rows, d_model)
-        hot_back = lax.all_to_all(hot_done.reshape(HOT, over_cap, d_model), 'ep', 0, 0, axis_index_groups=hot_lanes, tiled=True)
-        hot_back = hot_back.reshape(hot_rows, d_model)
+        hot_done = ffn(hot_recv.reshape(hot_count, d_model), hot_in, hot_out).astype(BF16)
+
+        back, hot_back = return_rows(group_size, done, hot_done.reshape(HOT, over_cap, d_model))
+        back = back.reshape(base_rows, d_model)
+        hot_back = hot_back.reshape(hot_count, d_model)
 
         shared_val = ffn(x_loc, shared_in, shared_out)
         routed = jnp.dot(base_gate, back, preferred_element_type=F32) + jnp.dot(hot_gate, hot_back, preferred_element_type=F32)

time: 1620 us -> 624 us (0.39)
  the two profiles are of different devices: /device:TPU:17 before, /device:TPU:30 now
where the time goes in v2:
time: 624 us; the launch traced here: 615 us
  Pallas kernels  488 us (78%)
  matrix products  70.3 us (11%)
  other arithmetic  28.1 us (5%)
  local copies, waits for them, and re-layouts  22.4 us (4%)
    pallas_call x1, Pallas kernels, dispatch_rows(): pl.pallas_call(functools.partial(dispatch_kernel, n, HOT), out_shape=(lik...  277 us
    pallas_call x1, Pallas kernels, return_rows(): pl.pallas_call(functools.partial(return_kernel, n, HOT), out_shape=(like(...  193 us
    dot_general x4, matrix products, ffn(): return jnp.dot(hidden, second, preferred_element_type=F32)  39.9 us
    pallas_call x1, Pallas kernels, exchange_counts(): pl.pallas_call(functools.partial(counts_kernel, n), out_shape=like(mine),...  18.3 us
  transfers between devices with their start and end apart: 2, of which 0 were waited for; matrix products, arithmetic and copies ran while one was open for 6% of the time, Pallas kernels for 3%

profile of v2, /device:TPU:30, one launch (start us, length us, event | category | flops | bytes accessed | tf_op | source)
XLA Modules:
  0.0 615.0 jit_solution(1719988177195519790)
XLA Ops:
  0.5 0.9 copy.66
  1.5 2.1 fusion.53
  3.6 0.6 convert_reduce_fusion
  4.3 18.3 %counts.1 = s32[2,128]{1,0:T(2,128)} custom-call(s32[2,128]{1,0:T(2,128)} %bitcast.104), custom_call_target="tpu_custom_call" | custom-call | tf_op jit(solution)/shard_map/counts/pallas_call | solution.py:160
  22.6 0.7 fusion.161
  23.6 5.7 fusion.107
  29.3 0.6 fusion.162
  30.5 0.8 fusion.142
  34.3 0.7 reduce_max.9
  36.6 0.7 select_reduce_fusion.1.source
  38.1 2.2 select_reduce_fusion
  40.4 2.9 convolution_convert_fusion.6
  43.3 1.3 convolution_compare_fusion
  44.7 9.6 %convolution_convert_fusion.2 = bf16[3072,2048]{1,0:T(8,128)(2,1)} fusion(pred[384,3072]{1,0:T(32,128)(4,1)S(1)} %convolution_compare_fusion, bf16[384,2048]{1,0:T(8,128)(2,1)S(1)} %copy-done.5), kind=kOutput, calls=%fused_computation.47 | convolution fusion | flops 4838129664 | bytes 15335424 | tf_op jit(solution)/shard_map/tr,tm->rm/dot_general | solution.py:291
  54.3 1.8 dynamic-slice_select_fusion
  56.1 2.6 select_n.148
  58.7 2.6 select_bitcast_fusion
  61.6 2.6 maximum_bitcast_fusion.slices
  64.1 276.8 %dispatch.1 = (bf16[128,24,2048]{2,1,0:T(8,128)(2,1)}, bf16[8,24,2048]{2,1,0:T(8,128)(2,1)}, bf16[128,8,2048]{2,1,0:T(8,128)(2,1)}) custom-call(s32[8]{0:T(128)} %select_reduce_fusion.1.source, bf16[128,24,2048]{2,1,0:T(8,128)(2,1)} %bitcast.96, bf16[8,24,2048]{2,1,0:T(8,128)(2,1)} %bitcast.101, bf16[128,8,2048]{2,1,0:T(8,128)(2,1)} %maximum_bitcast_fusion.slices), custom_call_target="tpu_custom_call" | custom-call | tf_op jit(solution)/shard_map/dispatch/pallas_call | solution.py:174
  341.0 1.8 slice.65
  342.8 2.6 reshape.208
  345.4 11.9 %fusion.163 = (bf16[128,16,2048]{2,1,0:T(8,128)(2,1)}, bf16[128,16,2048]{2,1,0:T(8,128)(2,1)}) fusion(bf16[128,24,2048]{2,1,0:T(8,128)(2,1)} %get-tuple-element.32), kind=kLoop, calls=%fused_computation.205 | loop fusion | bytes 33554432 | tf_op jit(solution)/shard_map/slice | solution.py:305
  357.3 15.0 %convolution_convert_fusion.4 = bf16[2048,2048]{1,0:T(8,128)(2,1)} fusion(bf16[2048,2048]{1,0:T(8,128)(2,1)} %bitcast.100, bf16[2,512,2048]{2,1,0:T(8,128)(2,1)} %param.13, bf16[2,2048,512]{2,1,0:T(8,128)(2,1)} %param.12), kind=kOutput, calls=%fused_computation.49 | convolution fusion | flops 8603566080 | bytes 20971520 | tf_op jit(solution)/shard_map/dot_general | solution.py:302
  372.3 15.2 %convolution_convert_fusion.3 = bf16[2048,2048]{1,0:T(8,128)(2,1)} fusion(bf16[2048,2048]{1,0:T(8,128)(2,1)} %bitcast.99, bf16[2,512,2048]{2,1,0:T(8,128)(2,1)} %param.13, bf16[2,2048,512]{2,1,0:T(8,128)(2,1)} %param.12), kind=kOutput, calls=%fused_computation.48 | convolution fusion | flops 8603566080 | bytes 20971520 | tf_op jit(solution)/shard_map/dot_general | solution.py:302
  387.5 3.9 convolution_convert_fusion.5
  391.4 6.4 %fusion.164 = (bf16[128,8,2048]{2,1,0:T(8,128)(2,1)S(1)}, bf16[128,8,2048]{2,1,0:T(8,128)(2,1)S(1)}, bf16[128,8,2048]{2,1,0:T(8,128)(2,1)S(1)}) fusion(bf16[128,16,2048]{2,1,0:T(8,128)(2,1)} %bitcast.97, bf16[128,16,2048]{2,1,0:T(8,128)(2,1)} %bitcast.98, pred[8]{0:T(512)(128)(4,1)S(1)} %iota_compare_fusion.17), kind=kLoop, calls=%fused_computation.206 | loop fusion | flops 2097152 | bytes 29360136 | tf_op jit(solution)/shard_map/slice | solution.py:310
  397.8 5.5 pad_maximum_fusion.rows
  403.3 192.6 %collect.1 = (bf16[128,24,2048]{2,1,0:T(8,128)(2,1)}, bf16[8,24,2048]{2,1,0:T(8,128)(2,1)}) custom-call(bf16[128,24,2048]{2,1,0:T(8,128)(2,1)} %pad_maximum_fusion.rows, bf16[8,24,2048]{2,1,0:T(8,128)(2,1)} %bitcast.102), custom_call_target="tpu_custom_call" | custom-call | tf_op jit(solution)/shard_map/collect/pallas_call | solution.py:191
  595.9 11.1 %fusion.90 = f32[384,2048]{1,0:T(8,128)} fusion(bf16[3072,2048]{1,0:T(8,128)(2,1)} %bitcast.105, pred[384,3072]{1,0:T(32,128)(4,1)} %copy-done.12, s32[3072]{0:T(1024)S(1)} %get-tuple-element.77, bf16[384,256]{1,0:T(8,128)(2,1)S(1)} %select_reduce_fusion), kind=kOutput, calls=%fused_computation.109 | convolution fusion | flops 5438963712 | bytes 17117184 | tf_op jit(solution)/shard_map/dot_general | solution.py:318
  607.0 4.8 add_convert_fusion
  611.8 1.1 conditional.1
  612.9 1.6 copy-done.1
  (47 shorter events, 3.0 us)
Async XLA Ops:
  0.0 23.5 %copy-start = (bf16[512,2048]{1,0:T(8,128)(2,1)S(1)}, bf16[512,2048]{1,0:T(8,128)(2,1)}, u32[]{:S(2)}) copy-start(bf16[512,2048]{1,0:T(8,128)(2,1)} %param.15) | copy-start | bytes 6291460
  0.0 54.3 %collective-permute-start = (bf16[2,2048,512]{2,1,0:T(8,128)(2,1)}, bf16[2,2048,512]{2,1,0:T(8,128)(2,1)}, u32[]{:S(2)}, u32[]{:S(2)}) collective-permute-start(bf16[2,2048,512]{2,1,0:T(8,128)(2,1)} %param.12), channel_id=1, source_target_pairs={{0,1},{1,0},{2,3},{3,2},{4,5},{5,4},{6,7},{7,6},{8,9},{9,8},{10,11... | collective-permute-start | bytes 12582920 | tf_op jit(solution)/shard_map/ppermute | solution.py:232
  0.0 58.7 %collective-permute-start.1 = (bf16[2,512,2048]{2,1,0:T(8,128)(2,1)}, bf16[2,512,2048]{2,1,0:T(8,128)(2,1)}, u32[]{:S(2)}, u32[]{:S(2)}) collective-permute-start(bf16[2,512,2048]{2,1,0:T(8,128)(2,1)} %param.13), channel_id=1, source_target_pairs={{0,1},{1,0},{2,3},{3,2},{4,5},{5,4},{6,7},{7,6},{8,9},{9,8},{10,11... | collective-permute-start | bytes 12582920 | tf_op jit(solution)/shard_map/ppermute | solution.py:233
  23.5 5.8 copy-start.10
  23.5 5.8 copy-start.11
  43.2 1.4 copy-start.5
  44.7 9.6 %copy-start.12 = (pred[384,3072]{1,0:T(32,128)(4,1)}, pred[384,3072]{1,0:T(32,128)(4,1)S(1)}, u32[]{:S(2)}) copy-start(pred[384,3072]{1,0:T(32,128)(4,1)S(1)} %convolution_compare_fusion) | copy-start | bytes 3538948
  44.7 9.6 %copy-start.7 = (bf16[2,2048,512]{2,1,0:T(8,128)(2,1)S(1)}, bf16[2,2048,512]{2,1,0:T(8,128)(2,1)}, u32[]{:S(2)}) copy-start(bf16[2,2048,512]{2,1,0:T(8,128)(2,1)} %param.12) | copy-start | bytes 12582916
  58.7 2.9 copy-start.3
  372.3 15.2 %copy-start.4 = (bf16[2048,512]{1,0:T(8,128)(2,1)S(1)}, bf16[2048,512]{1,0:T(8,128)(2,1)}, u32[]{:S(2)}) copy-start(bf16[2048,512]{1,0:T(8,128)(2,1)} %reshape.208) | copy-start | bytes 6291460
  595.9 11.1 %copy-start.6 = (bf16[384,2048]{1,0:T(8,128)(2,1)S(1)}, bf16[384,2048]{1,0:T(8,128)(2,1)}, u32[]{:S(2)}) copy-start(bf16[384,2048]{1,0:T(8,128)(2,1)} %param.9) | copy-start | bytes 4718596
  595.9 11.1 %copy-start.8 = (bf16[8,24,2048]{2,1,0:T(8,128)(2,1)S(1)}, bf16[8,24,2048]{2,1,0:T(8,128)(2,1)}, u32[]{:S(2)}) copy-start(bf16[8,24,2048]{2,1,0:T(8,128)(2,1)} %get-tuple-element.36) | copy-start | bytes 2359300
  595.9 11.1 %copy-start.9 = (s32[384,8]{0,1:T(8,128)S(1)}, s32[384,8]{0,1:T(8,128)}, u32[]{:S(2)}) copy-start(s32[384,8]{0,1:T(8,128)} %param.10) | copy-start | bytes 36868
  612.9 1.6 copy-start.1
